TPU v7x, 32 devices: a 4x4x1 block of a 4x4x8 slice. The times are simulated.
32 devices in a mesh: rep: 1 (over z), dp: 32 (over x, y, core).
Axes of the slice: x: 4, y: 4, z: 1, core: 2. Of those that a mesh axis runs over, the one named last changes fastest.
The devices are a block of a 4x4x8 slice.
Arguments:
- g_w_gate: bfloat16 [32, 2, 512, 4096], P(('rep', 'dp'))
- g_w_up: bfloat16 [32, 2, 512, 4096], P(('rep', 'dp'))
- g_w_down: bfloat16 [32, 2, 4096, 512], P(('rep', 'dp'))
- w_gate: bfloat16 [2, 512, 4096], replicated
- w_up: bfloat16 [2, 512, 4096], replicated
- w_down: bfloat16 [2, 4096, 512], replicated
- m_w_gate: float32 [2, 512, 4096], P(None, 'dp')
- m_w_up: float32 [2, 512, 4096], P(None, 'dp')
- m_w_down: float32 [2, 4096, 512], P(None, 'dp')
- v_w_gate: float32 [2, 512, 4096], P(None, 'dp')
- v_w_up: float32 [2, 512, 4096], P(None, 'dp')
- v_w_down: float32 [2, 4096, 512], P(None, 'dp')
Outputs:
- output 1: bfloat16 [2, 512, 4096], P('rep')
- output 2: bfloat16 [2, 512, 4096], P('rep')
- output 3: bfloat16 [2, 4096, 512], P('rep')
- output 4: float32 [2, 512, 4096], P('rep', 'dp')
- output 5: float32 [2, 512, 4096], P('rep', 'dp')
- output 6: float32 [2, 4096, 512], P('rep', 'dp')
- output 7: float32 [2, 512, 4096], P('rep', 'dp')
- output 8: float32 [2, 512, 4096], P('rep', 'dp')
- output 9: float32 [2, 4096, 512], P('rep', 'dp')
All inputs are finite; a program needn't handle non-finite values.
Results may differ from a plain program's by a relative error of at most 0.022.
Values are sent between devices in bfloat16 or wider.
A program may use at most 768 MiB of HBM per device.

v0:
```python
import jax
import jax.numpy as jnp
from jax import lax
from jax.sharding import PartitionSpec as P


def adamw(w, m, v, g):
    m = 0.9 * m + 0.1 * g
    v = 0.95 * v + 0.05 * g * g
    step = m * lax.rsqrt(v + 1e-8) + 0.1 * w
    return (w - 0.02 * step).astype(jnp.bfloat16), m, v


def clipped(gradients, sum_of_squares, count):
    factor = jnp.minimum(1.0, 0.5 * lax.rsqrt(sum_of_squares / count + 1e-30))
    return [g * factor for g in gradients]


def solution(mesh):
    def step(*arrays):
        terms, weights, m, v = (arrays[i : i + 3] for i in (0, 3, 6, 9))
        gradients = [lax.psum_scatter(t[0], "dp", scatter_dimension=1, tiled=True).astype(jnp.float32) for t in terms]
        squares = lax.psum(sum(jnp.sum(g * g) for g in gradients), "dp")
        gradients = clipped(gradients, squares, lax.psum(1, "dp") * sum(g.size for g in gradients))
        me = lax.axis_index("dp")
        own = [lax.dynamic_slice_in_dim(w, me * one.shape[1], one.shape[1], 1).astype(jnp.float32) for w, one in zip(weights, m, strict=True)]
        new = [adamw(w, m, v, g) for w, m, v, g in zip(own, m, v, gradients, strict=True)]
        whole = [lax.all_gather(one[0], "dp", axis=1, tiled=True) for one in new]
        return (*whole, *(one[1] for one in new), *(one[2] for one in new))

    all_of, cut = P(None, None, None), P(None, "dp", None)
    return jax.shard_map(
        step,
        mesh=mesh,
        in_specs=(P(("rep", "dp"), None, None, None),) * 3 + (all_of,) * 3 + (cut,) * 6,
        out_specs=(P("rep", None, None),) * 3 + (P("rep", "dp", None),) * 6,
        check_vma=False,
    )
```

profile of v0, /device:TPU:97, one launch (start us, length us, event | category | flops | bytes accessed | tf_op | source)
XLA Modules:
  0.0 501.4 jit_solution(12854235385573485514)
XLA Ops:
  7.2 0.1 reduce-scatter.4.cloned.1.call-start
  7.3 0.7 reduce-scatter.4.cloned.1.call-update
  8.0 0.1 reduce-scatter.6.cloned.1.call-start
  8.1 0.0 copy-start
  8.1 0.0 copy-start.1
  8.1 0.0 copy-start.2
  8.1 0.0 copy-start.3
  8.1 0.7 reduce-scatter.6.cloned.1.call-update
  8.8 0.0 copy-start.4
  8.8 0.0 copy-start.5
  8.8 0.1 reduce-scatter.8.cloned.1.call-start
  8.9 0.7 reduce-scatter.8.cloned.1.call-update
  9.6 0.1 all-gather.8.cloned.1.call-start
  9.7 89.1 %reduce-scatter.4.cloned.1.call-done = bf16[2,16,4096]{2,1,0:T(8,128)(2,1)} async-done(((bf16[2,512,4096]{2,1,0:T(8,128)(2,1)}), bf16[2,16,4096]{2,1,0:T(8,128)(2,1)}) %reduce-scatter.4.cloned.1.call-update) | async-done | bytes 262160 | tf_op jit(solution)/shard_map/reduce_scatter | solution.py:22
  98.8 1.7 fusion.9
  100.5 86.3 %reduce-scatter.6.cloned.1.call-done = bf16[2,16,4096]{2,1,0:T(8,128)(2,1)} async-done(((bf16[2,512,4096]{2,1,0:T(8,128)(2,1)}), bf16[2,16,4096]{2,1,0:T(8,128)(2,1)}) %reduce-scatter.6.cloned.1.call-update) | async-done | bytes 262160 | tf_op jit(solution)/shard_map/reduce_scatter | solution.py:22
  186.8 1.7 fusion.10
  189.7 85.0 %reduce-scatter.8.cloned.1.call-done = bf16[2,128,512]{2,1,0:T(8,128)(2,1)} async-done(((bf16[2,4096,512]{2,1,0:T(8,128)(2,1)}), bf16[2,128,512]{2,1,0:T(8,128)(2,1)}) %reduce-scatter.8.cloned.1.call-update) | async-done | bytes 262160 | tf_op jit(solution)/shard_map/reduce_scatter | solution.py:22
  274.8 1.7 fusion.11
  277.1 46.4 %psum.7 = f32[]{:T(128)} all-reduce(f32[]{:T(128)S(6)} %add.65), channel_id=1, replica_groups=mesh['rep'=1,'dp'=32] {'dp'}, use_global_device_ids=true, to_apply=%region_6.0 | all-reduce | flops 1 | bytes 8 | tf_op jit(solution)/shard_map/psum | solution.py:23
  324.3 0.0 copy-done
  324.3 0.0 copy-done.1
  324.3 2.2 fusion.17
  326.5 0.1 all-gather.8.cloned.1.call-update
  326.6 0.1 all-gather.4.cloned.1.call-start
  326.7 0.0 copy-done.2
  326.7 0.0 copy-done.3
  326.7 2.2 fusion.8
  328.9 0.1 all-gather.4.cloned.1.call-update
  329.0 0.1 all-gather.6.cloned.1.call-start
  329.0 0.0 copy-done.4
  329.1 0.0 copy-done.5
  329.1 2.2 fusion.14
  331.3 0.1 all-gather.6.cloned.1.call-update
  331.3 41.2 %all-gather.8.cloned.1.call-done = bf16[2,4096,512]{2,1,0:T(8,128)(2,1)} async-done(((bf16[2,128,512]{2,1,0:T(8,128)(2,1)}), bf16[2,4096,512]{2,1,0:T(8,128)(2,1)}) %all-gather.8.cloned.1.call-update) | async-done | bytes 8388624 | tf_op jit(solution)/shard_map/all_gather | solution.py:28
  372.5 49.5 %all-gather.4.cloned.1.call-done = bf16[2,512,4096]{2,1,0:T(8,128)(2,1)} async-done(((bf16[2,16,4096]{2,1,0:T(8,128)(2,1)}), bf16[2,512,4096]{2,1,0:T(8,128)(2,1)}) %all-gather.4.cloned.1.call-update) | async-done | bytes 8388624 | tf_op jit(solution)/shard_map/all_gather | solution.py:28
  422.0 49.5 %all-gather.6.cloned.1.call-done = bf16[2,512,4096]{2,1,0:T(8,128)(2,1)} async-done(((bf16[2,16,4096]{2,1,0:T(8,128)(2,1)}), bf16[2,512,4096]{2,1,0:T(8,128)(2,1)}) %all-gather.6.cloned.1.call-update) | async-done | bytes 8388624 | tf_op jit(solution)/shard_map/all_gather | solution.py:28
  471.5 7.9 %copy.24 = bf16[2,512,4096]{2,1,0:T(8,128)(2,1)} copy(bf16[2,512,4096]{2,1,0:T(8,128)(2,1)} %all-gather.4.cloned.1.call-done) | data formatting | bytes 16777216
  479.4 7.9 %copy.25 = bf16[2,512,4096]{2,1,0:T(8,128)(2,1)} copy(bf16[2,512,4096]{2,1,0:T(8,128)(2,1)} %all-gather.6.cloned.1.call-done) | data formatting | bytes 16777216
  487.2 7.3 %copy.26 = bf16[2,4096,512]{2,1,0:T(8,128)(2,1)} copy(bf16[2,4096,512]{2,1,0:T(8,128)(2,1)} %all-gather.8.cloned.1.call-done) | data formatting | bytes 16777216
Async XLA Ops:
  7.2 91.6 %reduce-scatter.4.cloned.1.call-start = ((), (), s32[]{:S(2)}) async-start(), calls=%async_computation.3 | async-start | bytes 8650752 | tf_op jit(solution)/shard_map/reduce_scatter | solution.py:22
  8.0 178.8 %reduce-scatter.6.cloned.1.call-start = ((), (), s32[]{:S(2)}) async-start(), calls=%async_computation.4 | async-start | bytes 8650752 | tf_op jit(solution)/shard_map/reduce_scatter | solution.py:22
  8.1 316.2 %copy-start = (f32[2,128,512]{2,1,0:T(8,128)S(1)}, f32[2,128,512]{2,1,0:T(8,128)}, u32[]{:S(2)}) copy-start(f32[2,128,512]{2,1,0:T(8,128)} %param.23) | copy-start | bytes 1572868
  8.1 316.2 %copy-start.1 = (f32[2,128,512]{2,1,0:T(8,128)S(1)}, f32[2,128,512]{2,1,0:T(8,128)}, u32[]{:S(2)}) copy-start(f32[2,128,512]{2,1,0:T(8,128)} %param.20) | copy-start | bytes 1572868
  8.1 318.6 %copy-start.2 = (f32[2,16,4096]{2,1,0:T(8,128)S(1)}, f32[2,16,4096]{2,1,0:T(8,128)}, u32[]{:S(2)}) copy-start(f32[2,16,4096]{2,1,0:T(8,128)} %param.21) | copy-start | bytes 1572868
  8.1 318.6 %copy-start.3 = (f32[2,16,4096]{2,1,0:T(8,128)S(1)}, f32[2,16,4096]{2,1,0:T(8,128)}, u32[]{:S(2)}) copy-start(f32[2,16,4096]{2,1,0:T(8,128)} %param.18) | copy-start | bytes 1572868
  8.8 320.2 %copy-start.4 = (f32[2,16,4096]{2,1,0:T(8,128)S(1)}, f32[2,16,4096]{2,1,0:T(8,128)}, u32[]{:S(2)}) copy-start(f32[2,16,4096]{2,1,0:T(8,128)} %param.22) | copy-start | bytes 1572868
  8.8 320.2 %copy-start.5 = (f32[2,16,4096]{2,1,0:T(8,128)S(1)}, f32[2,16,4096]{2,1,0:T(8,128)}, u32[]{:S(2)}) copy-start(f32[2,16,4096]{2,1,0:T(8,128)} %param.19) | copy-start | bytes 1572868
  8.8 266.0 %reduce-scatter.8.cloned.1.call-start = ((), (), s32[]{:S(2)}) async-start(), calls=%async_computation.5 | async-start | bytes 8650752 | tf_op jit(solution)/shard_map/reduce_scatter | solution.py:22
  9.6 362.9 %all-gather.8.cloned.1.call-start = ((), (), s32[]{:S(2)}) async-start(), calls=%async_computation.8 | async-start | bytes 8650752 | tf_op jit(solution)/shard_map/all_gather | solution.py:28
  326.6 95.4 %all-gather.4.cloned.1.call-start = ((), (), s32[]{:S(2)}) async-start(), calls=%async_computation.6 | async-start | bytes 8650752 | tf_op jit(solution)/shard_map/all_gather | solution.py:28
  329.0 142.5 %all-gather.6.cloned.1.call-start = ((), (), s32[]{:S(2)}) async-start(), calls=%async_computation.7 | async-start | bytes 8650752 | tf_op jit(solution)/shard_map/all_gather | solution.py:28
Sparse Core Ops, SparseCore 0:
  11.6 87.1 reduce-scatter.3
  102.3 84.4 reduce-scatter.5
  190.3 84.4 reduce-scatter.7
  326.7 45.7 all-gather.7
  375.1 46.8 all-gather.3
  424.6 46.8 all-gather.5
where the time goes:
time: 502 us; the launch traced here: 501 us
  waiting for transfers between devices  403 us (80%)
  blocking collectives  46.4 us (9%)
  local copies, waits for them, and re-layouts  23.1 us (5%)
  between operations  16.9 us (3%)
  other arithmetic  11.8 us (2%)
    reduce_scatter x3, waiting for transfers between devices, step(): lax.psum_scatter(t[0], 'dp', scatter_dimension=1, tiled=True)  260 us
    all_gather x3, waiting for transfers between devices, step(): whole = [lax.all_gather(one[0], 'dp', axis=1, tiled=True) for one in new]  140 us
    psum x1, blocking collectives, step(): squares = lax.psum(sum((jnp.sum(g * g) for g in gradients)), 'dp')  46.4 us
    unnamed x15, local copies, waits for them, and re-layouts  23.1 us
  transfers between devices with their start and end apart: 6, of which 6 were waited for; matrix products, arithmetic and copies ran while one was open for 2% of the time, Pallas kernels for 0%

commit v1 on v0

v1 whole, which is shorter than its diff:
```python
import functools
import math

import jax
import jax.numpy as jnp
from jax import lax
from jax.experimental import pallas as pl
from jax.experimental.pallas import tpu as pltpu
from jax.sharding import PartitionSpec as P

CORES = 2
ROWS, COLS = 16, 512


def strips(shape):
    rows, cols = shape
    if rows > ROWS:
        return rows // ROWS, lambda i: (pl.ds(pl.multiple_of(i * ROWS, ROWS), ROWS), slice(None))
    return cols // COLS, lambda i: (slice(None), pl.ds(pl.multiple_of(i * COLS, COLS), COLS))


def kernel(n, side, *refs):
    (t, w, m, v, o, mo, vo, ring, pair, kept, g, held) = (refs[3 * i : 3 * i + 3] for i in range(12))
    (
        parts, own_sem, mate_sem, ring_sem, pair_sem, part_sem, state_sem, back_sem,
        mate_out, ring_out, pair_out, part_out,
    ) = refs[36:]
    kinds, layers = range(3), range(2)
    f32, bf16 = jnp.float32, jnp.bfloat16

    me = lax.axis_index("dp")
    core, chip = lax.rem(me, CORES), lax.div(me, CORES)
    x, y = lax.div(chip, side), lax.rem(chip, side)
    a, b = x + core * (y - x), y + core * (x - y)
    mate = {"dp": me + 1 - 2 * core}

    def turn(i):
        return lax.rem(i + side, side)

    def place(a_, b_, core_=core):
        return a_ + core_ * (b_ - a_), b_ + core_ * (a_ - b_)

    def device(a_, b_):
        x_, y_ = place(a_, b_)
        return {"dp": (x_ * side + y_) * CORES + core}

    near_a = [device(turn(a + 1), b), device(turn(a - 1), b)]
    near_b = [device(a, turn(b + 1)), device(a, turn(b - 1))]

    def off(k):
        return 2 + k - 3 * (k // 2) - 2 * (k // 3)

    def role(d, s, k, a_, b_):
        step = 1 - 2 * d
        to = turn(a_ + (0 if s == 3 else step + step * (s == 0)))
        return (1 - d if s == 1 else d), to, turn(b_ + off(k))

    def block(j, layer, a_, b_):
        return o[j].at[(layer, *place(a_, b_), core)]

    def other(j, layer, a_, b_):
        return o[j].at[(layer, *place(a_, b_), 1 - core)]

    def load(s, k):
        for d in layers:
            layer, a_, b_ = role(d, s, k, a, b)
            for j in kinds:
                pltpu.make_async_copy(t[j].at[(layer, *place(a_, b_), core)], block(j, layer, a_, b_), own_sem.at[d, s, k, j]).start()

    def hand(s, k):
        for d in layers:
            layer, a_, b_ = role(d, s, k, b, a)
            at = place(a_, b_, 1 - core)
            for j in kinds:
                pltpu.make_async_remote_copy(
                    t[j].at[(layer, *at, 1 - core)], o[j].at[(layer, *at, core)], mate_out.at[j], mate_sem.at[d, s, k, j], device_id=mate
                ).start()

    def arrived(ref, sem):
        pltpu.make_async_copy(ref, ref, sem).wait()

    def send(src, dst, out_sem, sem, to):
        pltpu.make_async_remote_copy(src, dst, out_sem, sem, device_id=to).start()

    def total(j, d, s, k, more=(), into=None):
        layer, a_, b_ = role(d, s, k, a, b)
        mine, its = block(j, layer, a_, b_), other(j, layer, a_, b_)
        into = mine if into is None else into
        arrived(mine, own_sem.at[d, s, k, j])
        arrived(its, mate_sem.at[d, s, k, j])
        count, cut = strips(mine.shape)

        @pl.loop(0, count)
        def _(i):
            at = cut(i)
            so_far = mine[at].astype(f32) + its[at].astype(f32)
            for one in more:
                so_far += one[at].astype(f32)
            into[at] = so_far.astype(into.dtype)

        return mine

    for j in kinds:
        x_, y_ = place(a, b)
        pltpu.make_async_copy(w[j].at[:, x_, y_, core], held[j], state_sem.at[0, j]).start()

    @pl.loop(0, side)
    def _(k):
        load(0, k)

    barrier = pltpu.get_barrier_semaphore()
    for to in (*near_a, *near_b, mate):
        pl.semaphore_signal(barrier, inc=1, device_id=to)
    pl.semaphore_wait(barrier, 5)

    @pl.loop(0, side)
    def _(k):
        hand(0, k)

    for s in (1, 2, 3):
        pl.loop(0, side)(functools.partial(load, s))
    for j in kinds:
        pltpu.make_async_copy(m[j], mo[j], state_sem.at[1, j]).start()
        pltpu.make_async_copy(v[j], vo[j], state_sem.at[2, j]).start()

    for s in range(3):

        @pl.loop(0, side)
        def _(k, s=s):
            hand(s + 1, k)
            for j in kinds:
                for d in layers:
                    more = ()
                    if s == 2:
                        arrived(ring[j].at[d, 0, k], ring_sem.at[d, 0, k, j])
                        more = (ring[j].at[d, 0, k],)
                    mine = total(j, d, s, k, more)
                    send(mine, ring[j].at[d, s, k], ring_out.at[j], ring_sem.at[d, s, k, j], near_a[d])

    def last(j, layer, k, more=(), into=None):
        came = [ring[j].at[layer, 2, k], ring[j].at[1 - layer, 1, k]]
        arrived(came[0], ring_sem.at[layer, 2, k, j])
        arrived(came[1], ring_sem.at[1 - layer, 1, k, j])
        return total(j, layer, 3, k, (*came, *more), into)

    def onward(j, layer, k, d, s, more=()):
        send(last(j, layer, k, more), pair[j].at[d, s], pair_out.at[j], pair_sem.at[d, s, j], near_b[d])

    for j in kinds:
        for d in layers:
            onward(j, d, 0, d, 0)
    for j in kinds:
        onward(j, 0, 1, 1, 1)
        onward(j, 1, 2, 0, 1)
    for j in kinds:
        for layer, k, d in ((1, 1, 1), (0, 2, 0)):
            arrived(pair[j].at[d, 0], pair_sem.at[d, 0, j])
            onward(j, layer, k, d, 2, (pair[j].at[d, 0],))
    for j in kinds:
        for layer in layers:
            last(j, layer, 3, into=kept[j].at[layer])

    squares = jnp.zeros((ROWS, COLS), f32)
    for j in kinds:
        for layer in layers:
            came = [pair[j].at[layer, 2], pair[j].at[1 - layer, 1]]
            arrived(came[0], pair_sem.at[layer, 2, j])
            arrived(came[1], pair_sem.at[1 - layer, 1, j])
            count, cut = strips(came[0].shape)

            def finish(i, so_far, j=j, layer=layer, came=came, cut=cut):
                at = cut(i)
                grad = kept[j].at[layer][at] + came[0][at].astype(f32) + came[1][at].astype(f32)
                grad = grad.astype(bf16)
                g[j].at[layer][at] = grad
                grad = grad.astype(f32)
                return so_far + grad * grad

            squares = lax.fori_loop(0, count, finish, squares)
    by_lane = jnp.sum(squares, axis=0, keepdims=True)
    parts[me] = sum(by_lane[:, i * 128 : (i + 1) * 128] for i in range(COLS // 128))
    for j in kinds:
        arrived(ring[j], ring_out.at[j])
        arrived(pair[j], pair_out.at[j])
        arrived(o[j].at[:, :, :, 0], mate_out.at[j])

    @pl.loop(1, n)
    def _(i):
        send(parts.at[me], parts.at[me], part_out, part_sem, {"dp": lax.rem(me + i, n)})

    for j in kinds:
        arrived(held[j], state_sem.at[0, j])
        arrived(mo[j], state_sem.at[1, j])
        arrived(vo[j], state_sem.at[2, j])
    arrived(parts.at[pl.ds(0, n - 1)], part_sem)
    count = n * sum(math.prod(one.shape) for one in mo)
    whole = jnp.sum(jnp.sum(parts[...], axis=0), axis=1, keepdims=True)
    factor = jnp.minimum(1.0, 0.5 * lax.rsqrt(whole / count + 1e-30))

    def pass_on(j, layer, a_, b_, *, along_a=(), along_b=()):
        one = block(j, layer, a_, b_)
        for d, s in along_b:
            send(one, one, pair_out.at[j], pair_sem.at[d, s, j], near_b[d])
        for d, s, k in along_a:
            send(one, one, ring_out.at[j], ring_sem.at[d, s, k, j], near_a[d])
        send(one, one, mate_out.at[j], back_sem.at[j], mate)

    for layer in layers:
        for j in kinds:
            new = block(j, layer, a, b)
            count, cut = strips(new.shape)

            @pl.loop(0, count)
            def _(i, j=j, layer=layer, new=new, cut=cut):
                at = cut(i)
                grad = g[j].at[layer][at].astype(f32) * factor
                m_ = 0.9 * mo[j].at[layer][at] + 0.1 * grad
                v_ = 0.95 * vo[j].at[layer][at] + 0.05 * grad * grad
                w_ = held[j].at[layer][at].astype(f32)
                mo[j].at[layer][at] = m_
                vo[j].at[layer][at] = v_
                new[at] = (w_ - 0.02 * (m_ * lax.rsqrt(v_ + 1e-8) + 0.1 * w_)).astype(bf16)

            pass_on(j, layer, a, b, along_a=[(d, layer, 3) for d in layers], along_b=[(d, layer) for d in layers])

    def from_b(j, d, s):
        layer = d if s == 2 else s
        step = 1 - 2 * d
        b_ = turn(b - (2 if s == 2 else 1) * step)
        k = 0 if s == 2 else 1 + d
        arrived(block(j, layer, a, b_), pair_sem.at[d, s, j])
        pass_on(j, layer, a, b_, along_a=[(e, layer, k) for e in layers], along_b=[(d, 2)] if s == d else [])

    def from_a(j, d, s, k):
        layer = d if s == 2 else s
        step = 1 - 2 * d
        a_, b_ = turn(a - (2 if s == 2 else 1) * step), turn(b + off(k))
        arrived(block(j, layer, a_, b_), ring_sem.at[d, s, k, j])
        pass_on(j, layer, a_, b_, along_a=[(d, 2, k)] if s == d else [])

    for j in kinds:
        from_b(j, 0, 0)
        from_b(j, 1, 1)
        from_a(j, 0, 0, 3)
        from_a(j, 1, 1, 3)
    for j in kinds:
        from_b(j, 0, 1)
        from_b(j, 1, 0)
    for j in kinds:
        from_b(j, 0, 2)
        from_b(j, 1, 2)
    for k in range(3):
        for j in kinds:
            from_a(j, 0, 0, (1, 2, 0)[k])
            from_a(j, 1, 1, (2, 1, 0)[k])
    for k in (3, 1, 2, 0):
        for j in kinds:
            from_a(j, 0, 1, k)
            from_a(j, 1, 0, k)
    for k in (3, 1, 2, 0):
        for j in kinds:
            from_a(j, 0, 2, k)
            from_a(j, 1, 2, k)

    for j in kinds:
        arrived(o[j].at[:, :, :, 0], back_sem.at[j])
        arrived(o[j].at[:, :, :, 0], mate_out.at[j])
        arrived(ring[j], ring_out.at[j])
        arrived(pair[j], pair_out.at[j])
    arrived(parts.at[pl.ds(0, n - 1)], part_out)


def write_out(*refs):
    sem = refs[-1]
    moves = [pltpu.make_async_copy(src, dst, sem.at[i]) for i, (src, dst) in enumerate(zip(refs[:9], refs[9:18], strict=True))]
    for one in moves:
        one.start()
    for one in moves:
        one.wait()


def solution(mesh):
    n = mesh.shape["dp"]
    side = math.isqrt(n // CORES)

    def step(*arrays):
        terms, weights, ms, vs = (arrays[i : i + 3] for i in (0, 3, 6, 9))
        blocks = [(one.shape[0], side, side, CORES, *one.shape[1:]) for one in ms]
        terms = [one.reshape(s) for one, s in zip(terms, blocks, strict=True)]
        whole = [one.reshape(s) for one, s in zip(weights, blocks, strict=True)]
        f32, bf16 = jnp.float32, jnp.bfloat16
        dma = pltpu.SemaphoreType.DMA
        tail = [s[-2:] for s in blocks]
        out = pl.pallas_call(
            functools.partial(kernel, n, side),
            out_shape=[pltpu.VMEM(s, bf16) for s in blocks] + [pltpu.VMEM(one.shape, f32) for one in (*ms, *vs)],
            in_specs=[pl.BlockSpec(memory_space=pltpu.HBM)] * 12,
            out_specs=[pl.BlockSpec(memory_space=pltpu.VMEM)] * 9,
            scratch_shapes=[
                *(pltpu.VMEM((2, 3, side, *s), bf16) for s in tail),
                *(pltpu.VMEM((2, 3, *s), bf16) for s in tail),
                *(pltpu.VMEM(one.shape, f32) for one in ms),
                *(pltpu.VMEM(one.shape, bf16) for one in ms),
                *(pltpu.VMEM(one.shape, bf16) for one in ms),
                pltpu.VMEM((n, 1, 128), f32),
                dma((2, 4, side, 3)),
                dma((2, 4, side, 3)),
                dma((2, 3, side, 3)),
                dma((2, 3, 3)),
                dma(()),
                dma((3, 3)),
                dma((3,)),
                dma((3,)),
                dma((3,)),
                dma((3,)),
                dma(()),
            ],
            compiler_params=pltpu.CompilerParams(collective_id=0, has_side_effects=True, vmem_limit_bytes=24 << 20),
        )(*(pltpu.with_memory_space_constraint(one, pltpu.HBM) for one in (*terms, *whole, *ms, *vs)))
        out = pl.pallas_call(
            write_out,
            out_shape=[jax.ShapeDtypeStruct(one.shape, one.dtype) for one in out],
            in_specs=[pl.BlockSpec(memory_space=pltpu.VMEM)] * 9,
            out_specs=[pl.BlockSpec(memory_space=pltpu.HBM)] * 9,
            scratch_shapes=[dma((9,))],
            compiler_params=pltpu.CompilerParams(vmem_limit_bytes=1 << 20),
        )(*out)
        return (*(one.reshape(w.shape) for one, w in zip(out[:3], weights, strict=True)), *out[3:])

    all_of, cut = P(None, None, None), P(None, "dp", None)
    return jax.shard_map(
        step,
        mesh=mesh,
        in_specs=(P(("rep", "dp"), None, None, None),) * 3 + (all_of,) * 3 + (cut,) * 6,
        out_specs=(P("rep", None, None),) * 3 + (P("rep", "dp", None),) * 6,
        check_vma=False,
    )
```

time: 502 us -> 160 us (0.32)
  waiting for transfers between devices: 403 us -> 0 us
  Pallas kernels: 0 us -> 160 us
  blocking collectives: 46.4 us -> 0 us
  local copies, waits for them, and re-layouts: 23.1 us -> 0 us
  between operations: 16.9 us -> 0.65 us
  other arithmetic: 11.8 us -> 0 us
    reduce_scatter x3 -> x0, waiting for transfers between devices: 260 us -> none  [step(): lax.psum_scatter(t[0], 'dp', scatter_dimension=1, tiled=True)]
    pallas_call x0 -> x2, Pallas kernels: none -> 160 us  [the longest x1 150 us: step(): pl.pallas_call(functools.partial(kernel, n, side), out_shape=[pltpu.VMEM(...]
    all_gather x3 -> x0, waiting for transfers between devices: 140 us -> none  [step(): whole = [lax.all_gather(one[0], 'dp', axis=1, tiled=True) for one in new]]
    psum x1 -> x0, blocking collectives: 46.4 us -> none  [step(): squares = lax.psum(sum((jnp.sum(g * g) for g in gradients)), 'dp')]
    unnamed x15 -> x0, local copies, waits for them, and re-layouts: 23.1 us -> none
    convert_element_type x3 -> x0, other arithmetic: 6.68 us -> none  [adamw(): return ((w - 0.02 * step).astype(jnp.bfloat16), m, v)]
    reduce_sum x3 -> x0, other arithmetic: 5.07 us -> none  [step(): squares = lax.psum(sum((jnp.sum(g * g) for g in gradients)), 'dp')]
  transfers between devices with their start and end apart: 6 -> 0, of which waited for: 6 -> 0; matrix products, arithmetic and copies ran while one was open for 2% -> 0% of each run, Pallas kernels for 0% -> 0%
where the time goes in v1:
time: 160 us
  Pallas kernels  160 us (100%)
    pallas_call x1, Pallas kernels, step(): pl.pallas_call(functools.partial(kernel, n, side), out_shape=[pltpu.VMEM(...  150 us
    pallas_call x1, Pallas kernels, step(): pl.pallas_call(write_out, out_shape=[jax.ShapeDtypeStruct(one.shape, one....  9.47 us

profile of v1, /device:TPU:97, one launch (start us, length us, event | category | flops | bytes accessed | tf_op | source)
XLA Modules:
  0.0 160.2 jit_solution(10443760978491995276)
XLA Ops:
  0.6 150.0 %shard_map.187 = (bf16[2,4,4,2,16,4096]{5,4,3,2,1,0:T(8,128)(2,1)S(1)}, bf16[2,4,4,2,16,4096]{5,4,3,2,1,0:T(8,128)(2,1)S(1)}, bf16[2,4,4,2,128,512]{5,4,3,2,1,0:...) custom-call(bf16[2,4,4,2,16,4096]{5,4,3,2,1,0:T(8,128)(2,1)} %bitcas, ...), custom_call_target="tpu_custom_call" | custom-call | tf_op jit(solution)/shard_map/pallas_call | solution.py:294
  150.7 9.5 %shard_map.188 = (bf16[2,4,4,2,16,4096]{5,4,3,2,1,0:T(8,128)(2,1)}, bf16[2,4,4,2,16,4096]{5,4,3,2,1,0:T(8,128)(2,1)}, bf16[2,4,4,2,128,512]{5,4,3,2,1,0:T(8,128)...) custom-call(bf16[2,4,4,2,16,4096]{5,4,3,2,1,0:T(8,128)(2,1)S(1)} %ge, ...), custom_call_target="tpu_custom_call" | custom-call | tf_op jit(solution)/shard_map/pallas_call | solution.py:320

commit v2 on v1

--- a/solution.py
+++ b/solution.py
@@ -22,7 +22,7 @@
 def kernel(n, side, *refs):
     (t, w, m, v, o, mo, vo, ring, pair, kept, g, held) = (refs[3 * i : 3 * i + 3] for i in range(12))
     (
-        parts, own_sem, mate_sem, ring_sem, pair_sem, part_sem, state_sem, back_sem,
+        parts, own_sem, first_sem, mate_sem, ring_sem, pair_sem, part_sem, state_sem, back_sem,
         mate_out, ring_out, pair_out, part_out,
     ) = refs[36:]
     kinds, layers = range(3), range(2)
@@ -65,16 +65,18 @@
         for d in layers:
             layer, a_, b_ = role(d, s, k, a, b)
             for j in kinds:
-                pltpu.make_async_copy(t[j].at[(layer, *place(a_, b_), core)], block(j, layer, a_, b_), own_sem.at[d, s, k, j]).start()
-
-    def hand(s, k):
+                pltpu.make_async_copy(t[j].at[(layer, *place(a_, b_), core)], block(j, layer, a_, b_), own_sem.at[s]).start()
+
+    def for_mate(s, k):
         for d in layers:
             layer, a_, b_ = role(d, s, k, b, a)
             at = place(a_, b_, 1 - core)
             for j in kinds:
-                pltpu.make_async_remote_copy(
-                    t[j].at[(layer, *at, 1 - core)], o[j].at[(layer, *at, core)], mate_out.at[j], mate_sem.at[d, s, k, j], device_id=mate
-                ).start()
+                yield d, j, t[j].at[(layer, *at, 1 - core)], o[j].at[(layer, *at, core)]
+
+    def hand(s, k):
+        for _, j, src, dst in for_mate(s, k):
+            pltpu.make_async_remote_copy(src, dst, mate_out.at[j], mate_sem.at[s, k], device_id=mate).start()
 
     def arrived(ref, sem):
         pltpu.make_async_copy(ref, ref, sem).wait()
@@ -86,8 +88,6 @@
         layer, a_, b_ = role(d, s, k, a, b)
         mine, its = block(j, layer, a_, b_), other(j, layer, a_, b_)
         into = mine if into is None else into
-        arrived(mine, own_sem.at[d, s, k, j])
-        arrived(its, mate_sem.at[d, s, k, j])
         count, cut = strips(mine.shape)
 
         @pl.loop(0, count)
@@ -100,42 +100,47 @@
 
         return mine
 
-    for j in kinds:
-        x_, y_ = place(a, b)
-        pltpu.make_async_copy(w[j].at[:, x_, y_, core], held[j], state_sem.at[0, j]).start()
-
-    @pl.loop(0, side)
-    def _(k):
-        load(0, k)
-
     barrier = pltpu.get_barrier_semaphore()
-    for to in (*near_a, *near_b, mate):
+    for to in (mate, *near_a, *near_b):
         pl.semaphore_signal(barrier, inc=1, device_id=to)
+    for d, j, src, _ in for_mate(0, 0):
+        pltpu.make_async_copy(src, g[j].at[d], state_sem.at[0]).start()
+    pl.loop(0, side)(functools.partial(load, 0))
     pl.semaphore_wait(barrier, 5)
 
-    @pl.loop(0, side)
-    def _(k):
-        hand(0, k)
-
+    arrived(pair[0], state_sem.at[0])
+    for d, j, _, dst in for_mate(0, 0):
+        send(g[j].at[d], dst, mate_out.at[j], first_sem.at[d, j], mate)
+    pl.loop(1, side)(functools.partial(hand, 0))
     for s in (1, 2, 3):
         pl.loop(0, side)(functools.partial(load, s))
     for j in kinds:
-        pltpu.make_async_copy(m[j], mo[j], state_sem.at[1, j]).start()
-        pltpu.make_async_copy(v[j], vo[j], state_sem.at[2, j]).start()
-
-    for s in range(3):
-
-        @pl.loop(0, side)
-        def _(k, s=s):
-            hand(s + 1, k)
-            for j in kinds:
-                for d in layers:
-                    more = ()
-                    if s == 2:
-                        arrived(ring[j].at[d, 0, k], ring_sem.at[d, 0, k, j])
-                        more = (ring[j].at[d, 0, k],)
-                    mine = total(j, d, s, k, more)
-                    send(mine, ring[j].at[d, s, k], ring_out.at[j], ring_sem.at[d, s, k, j], near_a[d])
+        x_, y_ = place(a, b)
+        pltpu.make_async_copy(w[j].at[:, x_, y_, core], held[j], state_sem.at[0]).start()
+        pltpu.make_async_copy(m[j], mo[j], state_sem.at[1]).start()
+        pltpu.make_async_copy(v[j], vo[j], state_sem.at[2]).start()
+
+    def out_along_a(s, k, first=False):
+        if not first:
+            arrived(pair[0], mate_sem.at[s, k])
+        for j in kinds:
+            for d in layers:
+                more = ()
+                if first:
+                    arrived(g[j].at[d], first_sem.at[d, j])
+                if s == 2:
+                    arrived(ring[j].at[d, 0, k], ring_sem.at[d, 0, k, j])
+                    more = (ring[j].at[d, 0, k],)
+                mine = total(j, d, s, k, more)
+                send(mine, ring[j].at[d, s, k], ring_out.at[j], ring_sem.at[d, s, k, j], near_a[d])
+        hand(s + 1, k)
+
+    arrived(ring[0], own_sem.at[0])
+    out_along_a(0, 0, True)
+    pl.loop(1, side)(functools.partial(out_along_a, 0))
+    for s in (1, 2):
+        arrived(ring[0], own_sem.at[s])
+        pl.loop(0, side)(functools.partial(out_along_a, s))
 
     def last(j, layer, k, more=(), into=None):
         came = [ring[j].at[layer, 2, k], ring[j].at[1 - layer, 1, k]]
@@ -143,6 +148,10 @@
         arrived(came[1], ring_sem.at[1 - layer, 1, k, j])
         return total(j, layer, 3, k, (*came, *more), into)
 
+    arrived(ring[0], own_sem.at[3])
+    for k in range(side):
+        arrived(pair[0], mate_sem.at[3, k])
+
     def onward(j, layer, k, d, s, more=()):
         send(last(j, layer, k, more), pair[j].at[d, s], pair_out.at[j], pair_sem.at[d, s, j], near_b[d])
 
@@ -160,6 +169,8 @@
         for layer in layers:
             last(j, layer, 3, into=kept[j].at[layer])
 
+    for j in kinds:
+        arrived(o[j].at[:, :, :, 0], mate_out.at[j])
     squares = jnp.zeros((ROWS, COLS), f32)
     for j in kinds:
         for layer in layers:
@@ -182,16 +193,17 @@
     for j in kinds:
         arrived(ring[j], ring_out.at[j])
         arrived(pair[j], pair_out.at[j])
-        arrived(o[j].at[:, :, :, 0], mate_out.at[j])
-
-    @pl.loop(1, n)
+
+    far = CORES * (side + 1) * (side // 2)
+
+    @pl.loop(0, n - 1)
     def _(i):
-        send(parts.at[me], parts.at[me], part_out, part_sem, {"dp": lax.rem(me + i, n)})
-
-    for j in kinds:
-        arrived(held[j], state_sem.at[0, j])
-        arrived(mo[j], state_sem.at[1, j])
-        arrived(vo[j], state_sem.at[2, j])
+        ahead = lax.rem(far - 1 + i, n - 1) + 1
+        send(parts.at[me], parts.at[me], part_out, part_sem, {"dp": lax.rem(me + ahead, n)})
+
+    arrived(pair[0], state_sem.at[0])
+    arrived(ring[0].at[0], state_sem.at[1])
+    arrived(ring[0].at[0], state_sem.at[2])
     arrived(parts.at[pl.ds(0, n - 1)], part_sem)
     count = n * sum(math.prod(one.shape) for one in mo)
     whole = jnp.sum(jnp.sum(parts[...], axis=0), axis=1, keepdims=True)
@@ -303,12 +315,13 @@
                 *(pltpu.VMEM(one.shape, bf16) for one in ms),
                 *(pltpu.VMEM(one.shape, bf16) for one in ms),
                 pltpu.VMEM((n, 1, 128), f32),
-                dma((2, 4, side, 3)),
-                dma((2, 4, side, 3)),
+                dma((4,)),
+                dma((2, 3)),
+                dma((4, side)),
                 dma((2, 3, side, 3)),
                 dma((2, 3, 3)),
                 dma(()),
-                dma((3, 3)),
+                dma((3,)),
                 dma((3,)),
                 dma((3,)),
                 dma((3,)),

time: 160 us -> 159 us (level)
  Pallas kernels: 160 us -> 158 us
where the time goes in v2:
time: 159 us
  Pallas kernels  158 us (99%)
    pallas_call x1, Pallas kernels, step(): pl.pallas_call(functools.partial(kernel, n, side), out_shape=[pltpu.VMEM(...  149 us
    pallas_call x1, Pallas kernels, step(): pl.pallas_call(write_out, out_shape=[jax.ShapeDtypeStruct(one.shape, one....  9.47 us

profile of v2, /device:TPU:97, one launch (start us, length us, event | category | flops | bytes accessed | tf_op | source)
XLA Modules:
  0.0 158.8 jit_solution(1597199449680815096)
XLA Ops:
  0.6 148.7 %shard_map.187 = (bf16[2,4,4,2,16,4096]{5,4,3,2,1,0:T(8,128)(2,1)S(1)}, bf16[2,4,4,2,16,4096]{5,4,3,2,1,0:T(8,128)(2,1)S(1)}, bf16[2,4,4,2,128,512]{5,4,3,2,1,0:...) custom-call(bf16[2,4,4,2,16,4096]{5,4,3,2,1,0:T(8,128)(2,1)} %bitcas, ...), custom_call_target="tpu_custom_call" | custom-call | tf_op jit(solution)/shard_map/pallas_call | solution.py:306
  149.4 9.5 %shard_map.188 = (bf16[2,4,4,2,16,4096]{5,4,3,2,1,0:T(8,128)(2,1)}, bf16[2,4,4,2,16,4096]{5,4,3,2,1,0:T(8,128)(2,1)}, bf16[2,4,4,2,128,512]{5,4,3,2,1,0:T(8,128)...) custom-call(bf16[2,4,4,2,16,4096]{5,4,3,2,1,0:T(8,128)(2,1)S(1)} %ge, ...), custom_call_target="tpu_custom_call" | custom-call | tf_op jit(solution)/shard_map/pallas_call | solution.py:333

commit v3 on v2

--- a/solution.py
+++ b/solution.py
@@ -22,7 +22,7 @@
 def kernel(n, side, *refs):
     (t, w, m, v, o, mo, vo, ring, pair, kept, g, held) = (refs[3 * i : 3 * i + 3] for i in range(12))
     (
-        parts, own_sem, first_sem, mate_sem, ring_sem, pair_sem, part_sem, state_sem, back_sem,
+        parts, own_sem, first_sem, mate_sem, ring_sem, late_sem, pair_sem, part_sem, state_sem, back_sem,
         mate_out, ring_out, pair_out, part_out,
     ) = refs[36:]
     kinds, layers = range(3), range(2)
@@ -76,10 +76,19 @@
 
     def hand(s, k):
         for _, j, src, dst in for_mate(s, k):
-            pltpu.make_async_remote_copy(src, dst, mate_out.at[j], mate_sem.at[s, k], device_id=mate).start()
+            pltpu.make_async_remote_copy(src, dst, mate_out.at[j], mate_sem.at[3 + k if s == 0 else s - 1], device_id=mate).start()
 
     def arrived(ref, sem):
         pltpu.make_async_copy(ref, ref, sem).wait()
+
+    def along_a(j, d, s, k):
+        return late_sem.at[d, k, j] if s == 2 else ring_sem.at[d, s, k]
+
+    def arrived_a(ref, j, d, s, k):
+        if s == 2:
+            arrived(ref, late_sem.at[d, k, j])
+        elif j == 0:
+            arrived(pair[0].at[0], ring_sem.at[d, s, k])
 
     def send(src, dst, out_sem, sem, to):
         pltpu.make_async_remote_copy(src, dst, out_sem, sem, device_id=to).start()
@@ -90,7 +99,7 @@
         into = mine if into is None else into
         count, cut = strips(mine.shape)
 
-        @pl.loop(0, count)
+        @pl.loop(0, count, unroll=4)
         def _(i):
             at = cut(i)
             so_far = mine[at].astype(f32) + its[at].astype(f32)
@@ -112,45 +121,45 @@
     for d, j, _, dst in for_mate(0, 0):
         send(g[j].at[d], dst, mate_out.at[j], first_sem.at[d, j], mate)
     pl.loop(1, side)(functools.partial(hand, 0))
-    for s in (1, 2, 3):
-        pl.loop(0, side)(functools.partial(load, s))
-    for j in kinds:
-        x_, y_ = place(a, b)
-        pltpu.make_async_copy(w[j].at[:, x_, y_, core], held[j], state_sem.at[0]).start()
-        pltpu.make_async_copy(m[j], mo[j], state_sem.at[1]).start()
-        pltpu.make_async_copy(v[j], vo[j], state_sem.at[2]).start()
 
     def out_along_a(s, k, first=False):
-        if not first:
-            arrived(pair[0], mate_sem.at[s, k])
+        if s == 0 and not first:
+            arrived(pair[0], mate_sem.at[3 + k])
         for j in kinds:
             for d in layers:
                 more = ()
                 if first:
                     arrived(g[j].at[d], first_sem.at[d, j])
                 if s == 2:
-                    arrived(ring[j].at[d, 0, k], ring_sem.at[d, 0, k, j])
+                    arrived_a(ring[j].at[d, 0, k], j, d, 0, k)
                     more = (ring[j].at[d, 0, k],)
                 mine = total(j, d, s, k, more)
-                send(mine, ring[j].at[d, s, k], ring_out.at[j], ring_sem.at[d, s, k, j], near_a[d])
+                send(mine, ring[j].at[d, s, k], ring_out.at[j], along_a(j, d, s, k), near_a[d])
         hand(s + 1, k)
 
     arrived(ring[0], own_sem.at[0])
     out_along_a(0, 0, True)
+    for s in (1, 2, 3):
+        pl.loop(0, side)(functools.partial(load, s))
+    for j in kinds:
+        x_, y_ = place(a, b)
+        pltpu.make_async_copy(w[j].at[:, x_, y_, core], held[j], state_sem.at[0]).start()
+        pltpu.make_async_copy(m[j], mo[j], state_sem.at[1]).start()
+        pltpu.make_async_copy(v[j], vo[j], state_sem.at[2]).start()
     pl.loop(1, side)(functools.partial(out_along_a, 0))
     for s in (1, 2):
         arrived(ring[0], own_sem.at[s])
+        arrived(ring[0], mate_sem.at[s - 1])
         pl.loop(0, side)(functools.partial(out_along_a, s))
 
     def last(j, layer, k, more=(), into=None):
         came = [ring[j].at[layer, 2, k], ring[j].at[1 - layer, 1, k]]
-        arrived(came[0], ring_sem.at[layer, 2, k, j])
-        arrived(came[1], ring_sem.at[1 - layer, 1, k, j])
+        arrived_a(came[0], j, layer, 2, k)
+        arrived_a(came[1], j, 1 - layer, 1, k)
         return total(j, layer, 3, k, (*came, *more), into)
 
     arrived(ring[0], own_sem.at[3])
-    for k in range(side):
-        arrived(pair[0], mate_sem.at[3, k])
+    arrived(ring[0], mate_sem.at[2])
 
     def onward(j, layer, k, d, s, more=()):
         send(last(j, layer, k, more), pair[j].at[d, s], pair_out.at[j], pair_sem.at[d, s, j], near_b[d])
@@ -187,19 +196,16 @@
                 grad = grad.astype(f32)
                 return so_far + grad * grad
 
-            squares = lax.fori_loop(0, count, finish, squares)
+            squares = lax.fori_loop(0, count, finish, squares, unroll=4)
     by_lane = jnp.sum(squares, axis=0, keepdims=True)
     parts[me] = sum(by_lane[:, i * 128 : (i + 1) * 128] for i in range(COLS // 128))
     for j in kinds:
         arrived(ring[j], ring_out.at[j])
         arrived(pair[j], pair_out.at[j])
 
-    far = CORES * (side + 1) * (side // 2)
-
-    @pl.loop(0, n - 1)
+    @pl.loop(1, n)
     def _(i):
-        ahead = lax.rem(far - 1 + i, n - 1) + 1
-        send(parts.at[me], parts.at[me], part_out, part_sem, {"dp": lax.rem(me + ahead, n)})
+        send(parts.at[me], parts.at[me], part_out, part_sem, {"dp": lax.rem(me + i, n)})
 
     arrived(pair[0], state_sem.at[0])
     arrived(ring[0].at[0], state_sem.at[1])
@@ -209,12 +215,12 @@
     whole = jnp.sum(jnp.sum(parts[...], axis=0), axis=1, keepdims=True)
     factor = jnp.minimum(1.0, 0.5 * lax.rsqrt(whole / count + 1e-30))
 
-    def pass_on(j, layer, a_, b_, *, along_a=(), along_b=()):
+    def pass_on(j, layer, a_, b_, *, on_a=(), on_b=()):
         one = block(j, layer, a_, b_)
-        for d, s in along_b:
+        for d, s in on_b:
             send(one, one, pair_out.at[j], pair_sem.at[d, s, j], near_b[d])
-        for d, s, k in along_a:
-            send(one, one, ring_out.at[j], ring_sem.at[d, s, k, j], near_a[d])
+        for d, s, k in on_a:
+            send(one, one, ring_out.at[j], along_a(j, d, s, k), near_a[d])
         send(one, one, mate_out.at[j], back_sem.at[j], mate)
 
     for layer in layers:
@@ -222,7 +228,7 @@
             new = block(j, layer, a, b)
             count, cut = strips(new.shape)
 
-            @pl.loop(0, count)
+            @pl.loop(0, count, unroll=4)
             def _(i, j=j, layer=layer, new=new, cut=cut):
                 at = cut(i)
                 grad = g[j].at[layer][at].astype(f32) * factor
@@ -233,7 +239,7 @@
                 vo[j].at[layer][at] = v_
                 new[at] = (w_ - 0.02 * (m_ * lax.rsqrt(v_ + 1e-8) + 0.1 * w_)).astype(bf16)
 
-            pass_on(j, layer, a, b, along_a=[(d, layer, 3) for d in layers], along_b=[(d, layer) for d in layers])
+            pass_on(j, layer, a, b, on_a=[(d, layer, 3) for d in layers], on_b=[(d, layer) for d in layers])
 
     def from_b(j, d, s):
         layer = d if s == 2 else s
@@ -241,14 +247,14 @@
         b_ = turn(b - (2 if s == 2 else 1) * step)
         k = 0 if s == 2 else 1 + d
         arrived(block(j, layer, a, b_), pair_sem.at[d, s, j])
-        pass_on(j, layer, a, b_, along_a=[(e, layer, k) for e in layers], along_b=[(d, 2)] if s == d else [])
+        pass_on(j, layer, a, b_, on_a=[(e, layer, k) for e in layers], on_b=[(d, 2)] if s == d else [])
 
     def from_a(j, d, s, k):
         layer = d if s == 2 else s
         step = 1 - 2 * d
         a_, b_ = turn(a - (2 if s == 2 else 1) * step), turn(b + off(k))
-        arrived(block(j, layer, a_, b_), ring_sem.at[d, s, k, j])
-        pass_on(j, layer, a_, b_, along_a=[(d, 2, k)] if s == d else [])
+        arrived_a(block(j, layer, a_, b_), j, d, s, k)
+        pass_on(j, layer, a_, b_, on_a=[(d, 2, k)] if s == d else [])
 
     for j in kinds:
         from_b(j, 0, 0)
@@ -317,8 +323,9 @@
                 pltpu.VMEM((n, 1, 128), f32),
                 dma((4,)),
                 dma((2, 3)),
-                dma((4, side)),
-                dma((2, 3, side, 3)),
+                dma((3 + side,)),
+                dma((2, 2, side)),
+                dma((2, side, 3)),
                 dma((2, 3, 3)),
                 dma(()),
                 dma((3,)),

time: 159 us -> 158 us (level)
  no operation moved by 1% of the time
where the time goes in v3:
time: 158 us
  Pallas kernels  157 us (99%)
    pallas_call x1, Pallas kernels, step(): pl.pallas_call(functools.partial(kernel, n, side), out_shape=[pltpu.VMEM(...  148 us
    pallas_call x1, Pallas kernels, step(): pl.pallas_call(write_out, out_shape=[jax.ShapeDtypeStruct(one.shape, one....  9.47 us

profile of v3, /device:TPU:97, one launch (start us, length us, event | category | flops | bytes accessed | tf_op | source)
XLA Modules:
  0.0 157.9 jit_solution(3144376787637670796)
XLA Ops:
  0.6 147.8 %shard_map.187 = (bf16[2,4,4,2,16,4096]{5,4,3,2,1,0:T(8,128)(2,1)S(1)}, bf16[2,4,4,2,16,4096]{5,4,3,2,1,0:T(8,128)(2,1)S(1)}, bf16[2,4,4,2,128,512]{5,4,3,2,1,0:...) custom-call(bf16[2,4,4,2,16,4096]{5,4,3,2,1,0:T(8,128)(2,1)} %bitcas, ...), custom_call_target="tpu_custom_call" | custom-call | tf_op jit(solution)/shard_map/pallas_call | solution.py:312
  148.4 9.5 %shard_map.188 = (bf16[2,4,4,2,16,4096]{5,4,3,2,1,0:T(8,128)(2,1)}, bf16[2,4,4,2,16,4096]{5,4,3,2,1,0:T(8,128)(2,1)}, bf16[2,4,4,2,128,512]{5,4,3,2,1,0:T(8,128)...) custom-call(bf16[2,4,4,2,16,4096]{5,4,3,2,1,0:T(8,128)(2,1)S(1)} %ge, ...), custom_call_target="tpu_custom_call" | custom-call | tf_op jit(solution)/shard_map/pallas_call | solution.py:340

commit v4 on v3

--- a/solution.py
+++ b/solution.py
@@ -35,7 +35,7 @@
     mate = {"dp": me + 1 - 2 * core}
 
     def turn(i):
-        return lax.rem(i + side, side)
+        return lax.rem(i + 2 * side, side)
 
     def place(a_, b_, core_=core):
         return a_ + core_ * (b_ - a_), b_ + core_ * (a_ - b_)
@@ -44,14 +44,14 @@
         x_, y_ = place(a_, b_)
         return {"dp": (x_ * side + y_) * CORES + core}
 
-    near_a = [device(turn(a + 1), b), device(turn(a - 1), b)]
+    near_a = [device(turn(a - 1), b), device(turn(a + 1), b)]
     near_b = [device(a, turn(b + 1)), device(a, turn(b - 1))]
 
     def off(k):
         return 2 + k - 3 * (k // 2) - 2 * (k // 3)
 
     def role(d, s, k, a_, b_):
-        step = 1 - 2 * d
+        step = 2 * d - 1
         to = turn(a_ + (0 if s == 3 else step + step * (s == 0)))
         return (1 - d if s == 1 else d), to, turn(b_ + off(k))
 
@@ -68,11 +68,11 @@
                 pltpu.make_async_copy(t[j].at[(layer, *place(a_, b_), core)], block(j, layer, a_, b_), own_sem.at[s]).start()
 
     def for_mate(s, k):
-        for d in layers:
-            layer, a_, b_ = role(d, s, k, b, a)
-            at = place(a_, b_, 1 - core)
-            for j in kinds:
-                yield d, j, t[j].at[(layer, *at, 1 - core)], o[j].at[(layer, *at, core)]
+        at = [role(d, s, k, b, a) for d in layers]
+        for j in kinds:
+            for d in layers:
+                layer, to = at[d][0], place(*at[d][1:], 1 - core)
+                yield d, j, t[j].at[(layer, *to, 1 - core)], o[j].at[(layer, *to, core)]
 
     def hand(s, k):
         for _, j, src, dst in for_mate(s, k):
@@ -112,14 +112,11 @@
     barrier = pltpu.get_barrier_semaphore()
     for to in (mate, *near_a, *near_b):
         pl.semaphore_signal(barrier, inc=1, device_id=to)
-    for d, j, src, _ in for_mate(0, 0):
-        pltpu.make_async_copy(src, g[j].at[d], state_sem.at[0]).start()
     pl.loop(0, side)(functools.partial(load, 0))
     pl.semaphore_wait(barrier, 5)
 
-    arrived(pair[0], state_sem.at[0])
-    for d, j, _, dst in for_mate(0, 0):
-        send(g[j].at[d], dst, mate_out.at[j], first_sem.at[d, j], mate)
+    for d, j, src, dst in for_mate(0, 0):
+        send(src, dst, mate_out.at[j], first_sem.at[d, j], mate)
     pl.loop(1, side)(functools.partial(hand, 0))
 
     def out_along_a(s, k, first=False):
@@ -251,7 +248,7 @@
 
     def from_a(j, d, s, k):
         layer = d if s == 2 else s
-        step = 1 - 2 * d
+        step = 2 * d - 1
         a_, b_ = turn(a - (2 if s == 2 else 1) * step), turn(b + off(k))
         arrived_a(block(j, layer, a_, b_), j, d, s, k)
         pass_on(j, layer, a_, b_, on_a=[(d, 2, k)] if s == d else [])

time: 158 us -> 157 us (level)
  no operation moved by 1% of the time
where the time goes in v4:
time: 157 us
  Pallas kernels  157 us (100%)
    pallas_call x1, Pallas kernels, step(): pl.pallas_call(functools.partial(kernel, n, side), out_shape=[pltpu.VMEM(...  147 us
    pallas_call x1, Pallas kernels, step(): pl.pallas_call(write_out, out_shape=[jax.ShapeDtypeStruct(one.shape, one....  9.47 us

profile of v4, /device:TPU:97, one launch (start us, length us, event | category | flops | bytes accessed | tf_op | source)
XLA Modules:
  0.0 157.2 jit_solution(1678832919272115959)
XLA Ops:
  0.6 147.0 %shard_map.187 = (bf16[2,4,4,2,16,4096]{5,4,3,2,1,0:T(8,128)(2,1)S(1)}, bf16[2,4,4,2,16,4096]{5,4,3,2,1,0:T(8,128)(2,1)S(1)}, bf16[2,4,4,2,128,512]{5,4,3,2,1,0:...) custom-call(bf16[2,4,4,2,16,4096]{5,4,3,2,1,0:T(8,128)(2,1)} %bitcas, ...), custom_call_target="tpu_custom_call" | custom-call | tf_op jit(solution)/shard_map/pallas_call | solution.py:309
  147.7 9.5 %shard_map.188 = (bf16[2,4,4,2,16,4096]{5,4,3,2,1,0:T(8,128)(2,1)}, bf16[2,4,4,2,16,4096]{5,4,3,2,1,0:T(8,128)(2,1)}, bf16[2,4,4,2,128,512]{5,4,3,2,1,0:T(8,128)...) custom-call(bf16[2,4,4,2,16,4096]{5,4,3,2,1,0:T(8,128)(2,1)S(1)} %ge, ...), custom_call_target="tpu_custom_call" | custom-call | tf_op jit(solution)/shard_map/pallas_call | solution.py:337

commit v5 on v4

--- a/solution.py
+++ b/solution.py
@@ -200,7 +200,7 @@
         arrived(ring[j], ring_out.at[j])
         arrived(pair[j], pair_out.at[j])
 
-    @pl.loop(1, n)
+    @pl.loop(1, n, unroll=True)
     def _(i):
         send(parts.at[me], parts.at[me], part_out, part_sem, {"dp": lax.rem(me + i, n)})
 

time: 157 us -> 157 us (level)
  no operation moved by 1% of the time
where the time goes in v5:
time: 157 us
  Pallas kernels  156 us (99%)
    pallas_call x1, Pallas kernels, step(): pl.pallas_call(functools.partial(kernel, n, side), out_shape=[pltpu.VMEM(...  147 us
    pallas_call x1, Pallas kernels, step(): pl.pallas_call(write_out, out_shape=[jax.ShapeDtypeStruct(one.shape, one....  9.47 us

profile of v5, /device:TPU:97, one launch (start us, length us, event | category | flops | bytes accessed | tf_op | source)
XLA Modules:
  0.0 157.0 jit_solution(10875748875684563941)
XLA Ops:
  0.6 146.9 %shard_map.187 = (bf16[2,4,4,2,16,4096]{5,4,3,2,1,0:T(8,128)(2,1)S(1)}, bf16[2,4,4,2,16,4096]{5,4,3,2,1,0:T(8,128)(2,1)S(1)}, bf16[2,4,4,2,128,512]{5,4,3,2,1,0:...) custom-call(bf16[2,4,4,2,16,4096]{5,4,3,2,1,0:T(8,128)(2,1)} %bitcas, ...), custom_call_target="tpu_custom_call" | custom-call | tf_op jit(solution)/shard_map/pallas_call | solution.py:309
  147.5 9.5 %shard_map.188 = (bf16[2,4,4,2,16,4096]{5,4,3,2,1,0:T(8,128)(2,1)}, bf16[2,4,4,2,16,4096]{5,4,3,2,1,0:T(8,128)(2,1)}, bf16[2,4,4,2,128,512]{5,4,3,2,1,0:T(8,128)...) custom-call(bf16[2,4,4,2,16,4096]{5,4,3,2,1,0:T(8,128)(2,1)S(1)} %ge, ...), custom_call_target="tpu_custom_call" | custom-call | tf_op jit(solution)/shard_map/pallas_call | solution.py:337

commit v6 on v5

--- a/solution.py
+++ b/solution.py
@@ -23,7 +23,7 @@
     (t, w, m, v, o, mo, vo, ring, pair, kept, g, held) = (refs[3 * i : 3 * i + 3] for i in range(12))
     (
         parts, own_sem, first_sem, mate_sem, ring_sem, late_sem, pair_sem, part_sem, state_sem, back_sem,
-        mate_out, ring_out, pair_out, part_out,
+        mate_out, ring_out, pair_out, part_out, tail_sem, head_sem,
     ) = refs[36:]
     kinds, layers = range(3), range(2)
     f32, bf16 = jnp.float32, jnp.bfloat16
@@ -246,12 +246,33 @@
         arrived(block(j, layer, a, b_), pair_sem.at[d, s, j])
         pass_on(j, layer, a, b_, on_a=[(e, layer, k) for e in layers], on_b=[(d, 2)] if s == d else [])
 
+    def halves(one):
+        rows = one.shape[0]
+        part = rows * 5 // 8
+        return one.at[pl.ds(0, part)], one.at[pl.ds(part, rows - part)]
+
+    across_a = [{"dp": to["dp"] + 1 - 2 * core} for to in near_a]
+
     def from_a(j, d, s, k):
         layer = d if s == 2 else s
         step = 2 * d - 1
         a_, b_ = turn(a - (2 if s == 2 else 1) * step), turn(b + off(k))
-        arrived_a(block(j, layer, a_, b_), j, d, s, k)
-        pass_on(j, layer, a_, b_, on_a=[(d, 2, k)] if s == d else [])
+        one = block(j, layer, a_, b_)
+        is_last = (j, k) == (2, 0)
+        if s == 2 and is_last:
+            head, rest = halves(one)
+            arrived(head, late_sem.at[d, k, j])
+            send(head, head, ring_out.at[3], head_sem.at[d], mate)
+            arrived(rest, tail_sem.at[d, 0])
+            return
+        arrived_a(one, j, d, s, k)
+        pass_on(j, layer, a_, b_, on_a=[(d, 2, k)] if s == d and not is_last else [])
+        if s == d and is_last:
+            head, rest = halves(one)
+            send(head, head, ring_out.at[j], late_sem.at[d, k, j], near_a[d])
+            for other_core in (1 - core, core):
+                to = {"dp": near_a[d]["dp"] + other_core * (across_a[d]["dp"] - near_a[d]["dp"])}
+                send(rest, rest, ring_out.at[j + other_core], tail_sem.at[d, other_core], to)
 
     for j in kinds:
         from_b(j, 0, 0)
@@ -277,9 +298,17 @@
             from_a(j, 0, 2, k)
             from_a(j, 1, 2, k)
 
-    for j in kinds:
-        arrived(o[j].at[:, :, :, 0], back_sem.at[j])
-        arrived(o[j].at[:, :, :, 0], mate_out.at[j])
+    for d in layers:
+        head, rest = halves(block(2, d, a, b))
+        arrived(head, head_sem.at[d])
+        arrived(rest, tail_sem.at[d, 1])
+    arrived(pair[2].at[0, pl.ds(0, 2)], ring_out.at[3])
+    for j in kinds:
+        half = o[j].at[:, :, :, 0]
+        if j == 2:
+            half = o[j].at[:, :, :, 0, pl.ds(0, half.shape[-2] * 15 // 16)]
+        arrived(half, back_sem.at[j])
+        arrived(half, mate_out.at[j])
         arrived(ring[j], ring_out.at[j])
         arrived(pair[j], pair_out.at[j])
     arrived(parts.at[pl.ds(0, n - 1)], part_out)
@@ -328,9 +357,11 @@
                 dma((3,)),
                 dma((3,)),
                 dma((3,)),
-                dma((3,)),
+                dma((4,)),
                 dma((3,)),
                 dma(()),
+                dma((2, 2)),
+                dma((2,)),
             ],
             compiler_params=pltpu.CompilerParams(collective_id=0, has_side_effects=True, vmem_limit_bytes=24 << 20),
         )(*(pltpu.with_memory_space_constraint(one, pltpu.HBM) for one in (*terms, *whole, *ms, *vs)))

time: 157 us -> 157 us (level)
  no operation moved by 1% of the time
where the time goes in v6:
time: 157 us
  Pallas kernels  156 us (99%)
    pallas_call x1, Pallas kernels, step(): pl.pallas_call(functools.partial(kernel, n, side), out_shape=[pltpu.VMEM(...  147 us
    pallas_call x1, Pallas kernels, step(): pl.pallas_call(write_out, out_shape=[jax.ShapeDtypeStruct(one.shape, one....  9.47 us

profile of v6, /device:TPU:97, one launch (start us, length us, event | category | flops | bytes accessed | tf_op | source)
XLA Modules:
  0.0 156.8 jit_solution(2142004336351273639)
XLA Ops:
  0.6 146.7 %shard_map.187 = (bf16[2,4,4,2,16,4096]{5,4,3,2,1,0:T(8,128)(2,1)S(1)}, bf16[2,4,4,2,16,4096]{5,4,3,2,1,0:T(8,128)(2,1)S(1)}, bf16[2,4,4,2,128,512]{5,4,3,2,1,0:...) custom-call(bf16[2,4,4,2,16,4096]{5,4,3,2,1,0:T(8,128)(2,1)} %bitcas, ...), custom_call_target="tpu_custom_call" | custom-call | tf_op jit(solution)/shard_map/pallas_call | solution.py:338
  147.4 9.5 %shard_map.188 = (bf16[2,4,4,2,16,4096]{5,4,3,2,1,0:T(8,128)(2,1)}, bf16[2,4,4,2,16,4096]{5,4,3,2,1,0:T(8,128)(2,1)}, bf16[2,4,4,2,128,512]{5,4,3,2,1,0:T(8,128)...) custom-call(bf16[2,4,4,2,16,4096]{5,4,3,2,1,0:T(8,128)(2,1)S(1)} %ge, ...), custom_call_target="tpu_custom_call" | custom-call | tf_op jit(solution)/shard_map/pallas_call | solution.py:368

commit v7 on v6

--- a/solution.py
+++ b/solution.py
@@ -22,8 +22,8 @@
 def kernel(n, side, *refs):
     (t, w, m, v, o, mo, vo, ring, pair, kept, g, held) = (refs[3 * i : 3 * i + 3] for i in range(12))
     (
-        parts, own_sem, first_sem, mate_sem, ring_sem, late_sem, pair_sem, part_sem, state_sem, back_sem,
-        mate_out, ring_out, pair_out, part_out, tail_sem, head_sem,
+        parts, own_sem, first_sem, mate_sem, ring_sem, late_sem, pair_sem, part_sem, state_sem,
+        mate_out, ring_out, pair_out, part_out,
     ) = refs[36:]
     kinds, layers = range(3), range(2)
     f32, bf16 = jnp.float32, jnp.bfloat16
@@ -76,7 +76,7 @@
 
     def hand(s, k):
         for _, j, src, dst in for_mate(s, k):
-            pltpu.make_async_remote_copy(src, dst, mate_out.at[j], mate_sem.at[3 + k if s == 0 else s - 1], device_id=mate).start()
+            pltpu.make_async_remote_copy(src, dst, mate_out.at[j], mate_sem.at[2 + k if s == 0 else s - 1], device_id=mate).start()
 
     def arrived(ref, sem):
         pltpu.make_async_copy(ref, ref, sem).wait()
@@ -121,7 +121,7 @@
 
     def out_along_a(s, k, first=False):
         if s == 0 and not first:
-            arrived(pair[0], mate_sem.at[3 + k])
+            arrived(pair[0], mate_sem.at[2 + k])
         for j in kinds:
             for d in layers:
                 more = ()
@@ -218,14 +218,14 @@
             send(one, one, pair_out.at[j], pair_sem.at[d, s, j], near_b[d])
         for d, s, k in on_a:
             send(one, one, ring_out.at[j], along_a(j, d, s, k), near_a[d])
-        send(one, one, mate_out.at[j], back_sem.at[j], mate)
+        send(one, one, mate_out.at[j], own_sem.at[j], mate)
 
     for layer in layers:
         for j in kinds:
             new = block(j, layer, a, b)
             count, cut = strips(new.shape)
 
-            @pl.loop(0, count, unroll=4)
+            @pl.loop(0, count, unroll=8)
             def _(i, j=j, layer=layer, new=new, cut=cut):
                 at = cut(i)
                 grad = g[j].at[layer][at].astype(f32) * factor
@@ -262,8 +262,8 @@
         if s == 2 and is_last:
             head, rest = halves(one)
             arrived(head, late_sem.at[d, k, j])
-            send(head, head, ring_out.at[3], head_sem.at[d], mate)
-            arrived(rest, tail_sem.at[d, 0])
+            send(head, head, ring_out.at[3], first_sem.at[d, 2], mate)
+            arrived(rest, first_sem.at[d, 0])
             return
         arrived_a(one, j, d, s, k)
         pass_on(j, layer, a_, b_, on_a=[(d, 2, k)] if s == d and not is_last else [])
@@ -272,7 +272,7 @@
             send(head, head, ring_out.at[j], late_sem.at[d, k, j], near_a[d])
             for other_core in (1 - core, core):
                 to = {"dp": near_a[d]["dp"] + other_core * (across_a[d]["dp"] - near_a[d]["dp"])}
-                send(rest, rest, ring_out.at[j + other_core], tail_sem.at[d, other_core], to)
+                send(rest, rest, ring_out.at[j + other_core], first_sem.at[d, other_core], to)
 
     for j in kinds:
         from_b(j, 0, 0)
@@ -300,14 +300,14 @@
 
     for d in layers:
         head, rest = halves(block(2, d, a, b))
-        arrived(head, head_sem.at[d])
-        arrived(rest, tail_sem.at[d, 1])
+        arrived(head, first_sem.at[d, 2])
+        arrived(rest, first_sem.at[d, 1])
     arrived(pair[2].at[0, pl.ds(0, 2)], ring_out.at[3])
     for j in kinds:
         half = o[j].at[:, :, :, 0]
         if j == 2:
             half = o[j].at[:, :, :, 0, pl.ds(0, half.shape[-2] * 15 // 16)]
-        arrived(half, back_sem.at[j])
+        arrived(half, own_sem.at[j])
         arrived(half, mate_out.at[j])
         arrived(ring[j], ring_out.at[j])
         arrived(pair[j], pair_out.at[j])
@@ -349,19 +349,16 @@
                 pltpu.VMEM((n, 1, 128), f32),
                 dma((4,)),
                 dma((2, 3)),
-                dma((3 + side,)),
+                dma((2 + side,)),
                 dma((2, 2, side)),
                 dma((2, side, 3)),
                 dma((2, 3, 3)),
                 dma(()),
                 dma((3,)),
                 dma((3,)),
-                dma((3,)),
                 dma((4,)),
                 dma((3,)),
                 dma(()),
-                dma((2, 2)),
-                dma((2,)),
             ],
             compiler_params=pltpu.CompilerParams(collective_id=0, has_side_effects=True, vmem_limit_bytes=24 << 20),
         )(*(pltpu.with_memory_space_constraint(one, pltpu.HBM) for one in (*terms, *whole, *ms, *vs)))

time: 157 us -> 157 us (level)
  no operation moved by 1% of the time
where the time goes in v7:
time: 157 us
  Pallas kernels  156 us (99%)
    pallas_call x1, Pallas kernels, step(): pl.pallas_call(functools.partial(kernel, n, side), out_shape=[pltpu.VMEM(...  147 us
    pallas_call x1, Pallas kernels, step(): pl.pallas_call(write_out, out_shape=[jax.ShapeDtypeStruct(one.shape, one....  9.47 us

profile of v7, /device:TPU:97, one launch (start us, length us, event | category | flops | bytes accessed | tf_op | source)
XLA Modules:
  0.0 156.7 jit_solution(3618106356857405319)
XLA Ops:
  0.6 146.6 %shard_map.187 = (bf16[2,4,4,2,16,4096]{5,4,3,2,1,0:T(8,128)(2,1)S(1)}, bf16[2,4,4,2,16,4096]{5,4,3,2,1,0:T(8,128)(2,1)S(1)}, bf16[2,4,4,2,128,512]{5,4,3,2,1,0:...) custom-call(bf16[2,4,4,2,16,4096]{5,4,3,2,1,0:T(8,128)(2,1)} %bitcas, ...), custom_call_target="tpu_custom_call" | custom-call | tf_op jit(solution)/shard_map/pallas_call | solution.py:338
  147.2 9.5 %shard_map.188 = (bf16[2,4,4,2,16,4096]{5,4,3,2,1,0:T(8,128)(2,1)}, bf16[2,4,4,2,16,4096]{5,4,3,2,1,0:T(8,128)(2,1)}, bf16[2,4,4,2,128,512]{5,4,3,2,1,0:T(8,128)...) custom-call(bf16[2,4,4,2,16,4096]{5,4,3,2,1,0:T(8,128)(2,1)S(1)} %ge, ...), custom_call_target="tpu_custom_call" | custom-call | tf_op jit(solution)/shard_map/pallas_call | solution.py:365
